TPU v7x, 128 devices: a whole 4x4x4 slice. The times are simulated.
128 devices in a mesh: rad: 16 (over y, x), ang: 8 (over z, core).
Axes of the slice: x: 4, y: 4, z: 4, core: 2. Of those that a mesh axis runs over, the one named last changes fastest.
Arguments:
- density: float32 [3, 1024, 256, 512], P(None, 'rad', 'ang'), may hold values from -13 to 13
Outputs:
- potential: float32 [3, 1024, 256, 512], P(None, 'rad', 'ang')
All inputs are finite; a program needn't handle non-finite values.
Results may differ from a plain program's by a relative error of at most 0.0003.
Values sent between devices are 32-bit elements; how exact they have to be, the bound alone decides.
A program may use at most 128 MiB of HBM per device.

v0:
```python
import math

import jax
import jax.numpy as jnp
import numpy as np
from jax import lax
from jax.sharding import PartitionSpec as P

LMAX = 12


INNER = 0.5
COUPLING = 2000.0


def over_pieces(value, axis):
    return lax.all_gather(value, axis).sum(0)


def laid_out(parts, dim):
    parts = jnp.moveaxis(parts, 0, dim)
    dims = parts.shape
    return parts.reshape(*dims[:dim], dims[dim] * dims[dim + 1], *dims[dim + 2 :])


def from_everyone(value, axis):
    count = lax.axis_size(axis)
    return lax.all_to_all(
        jnp.broadcast_to(value[None], (count, *value.shape)), axis, 0, 0, tiled=True
    )


def gathered_copies(value, axis, dim):
    return laid_out(from_everyone(value, axis), dim)


def legendre_table(polar_angle):
    cos_theta = jnp.cos(polar_angle)
    sine_theta = jnp.sin(polar_angle)
    values_lm = {}
    values_lm[0, 0] = jnp.full_like(polar_angle, 1.0 / math.sqrt(4.0 * math.pi))
    for m in range(1, LMAX + 1):
        values_lm[m, m] = (
            math.sqrt((2.0 * m + 1.0) / (2.0 * m)) * sine_theta * values_lm[m - 1, m - 1]
        )
    for m in range(0, LMAX):
        values_lm[m + 1, m] = math.sqrt(2.0 * m + 3.0) * cos_theta * values_lm[m, m]
    for m in range(0, LMAX + 1):
        for l in range(m + 2, LMAX + 1):
            coef_a = math.sqrt((4.0 * l * l - 1.0) / (l * l - m * m))
            coef_b = math.sqrt(((l - 1.0) ** 2 - m * m) / (4.0 * (l - 1.0) ** 2 - 1.0))
            values_lm[l, m] = coef_a * (
                cos_theta * values_lm[l - 1, m] - coef_b * values_lm[l - 2, m]
            )
    degree_rows = []
    for l in range(LMAX + 1):
        columns = []
        for k in range(2 * LMAX + 1):
            m = (k + 1) // 2
            columns.append(values_lm[l, m] if m <= l else jnp.zeros_like(polar_angle))
        degree_rows.append(jnp.stack(columns, -1))
    return jnp.stack(degree_rows, 1)


def fourier_table(phi_cells):
    azimuth = jnp.arange(phi_cells, dtype=jnp.float32) * (2.0 * math.pi / phi_cells)
    column = jnp.arange(2 * LMAX + 1)
    order_m = ((column + 1) // 2).astype(jnp.float32)
    phase = azimuth[:, None] * order_m[None, :]
    root_two = math.sqrt(2.0)
    return jnp.where(
        column[None, :] == 0,
        jnp.ones_like(phase),
        jnp.where(column[None, :] % 2 == 1, root_two * jnp.cos(phase), root_two * jnp.sin(phase)),
    )


def slot_selector():
    width = 2 * LMAX + 1
    used = [l * width + k for l in range(LMAX + 1) for k in range(width) if (k + 1) // 2 <= l]
    table = np.zeros(((LMAX + 1) * width, len(used)), np.float32)
    table[np.array(used), np.arange(len(used))] = 1.0
    return jnp.asarray(table)


def body(density):
    snapshots, shells, theta_rows, phi_cells = density.shape
    width = 2 * LMAX + 1
    total_shells = shells * lax.axis_size("rad")
    total_rows = theta_rows * lax.axis_size("ang")
    row_index = lax.axis_index("ang") * theta_rows + jnp.arange(theta_rows, dtype=jnp.int32)
    polar_angle = (row_index.astype(jnp.float32) + 0.5) * (math.pi / total_rows)
    legendre = legendre_table(polar_angle)
    weights = jnp.sin(polar_angle) * (math.pi / total_rows) * (2.0 * math.pi / phi_cells)
    fourier = fourier_table(phi_cells)
    spacing = (1.0 - INNER) / total_shells
    shell_index = lax.axis_index("rad") * shells + jnp.arange(shells, dtype=jnp.int32)
    radius = INNER + (shell_index.astype(jnp.float32) + 0.5) * spacing
    azimuthal = jnp.dot(
        density.reshape(snapshots * shells * theta_rows, phi_cells),
        fourier,
        precision=lax.Precision.HIGHEST,
        preferred_element_type=jnp.float32,
    )
    azimuthal = azimuthal.reshape(snapshots, shells, theta_rows, width)
    partial_moments = jnp.einsum(
        "frtk,tlk->frlk",
        azimuthal,
        legendre * weights[:, None, None],
        precision=lax.Precision.HIGHEST,
    )
    selector = slot_selector()
    packed = jnp.dot(
        partial_moments.reshape(snapshots * shells, (LMAX + 1) * width),
        selector,
        precision=lax.Precision.HIGHEST,
        preferred_element_type=jnp.float32,
    )
    summed = over_pieces(packed, "ang")
    moments = jnp.dot(
        summed, selector.T, precision=lax.Precision.HIGHEST, preferred_element_type=jnp.float32
    ).reshape(snapshots, shells, LMAX + 1, width)
    degree = jnp.arange(LMAX + 1, dtype=jnp.float32)
    inner_terms = moments * (radius[:, None] ** (degree + 2.0) * spacing)[None, :, :, None]
    outer_terms = moments * (radius[:, None] ** (1.0 - degree) * spacing)[None, :, :, None]
    inner_total = jnp.sum(inner_terms, 1)
    outer_total = jnp.sum(outer_terms, 1)
    stacked = jnp.stack([inner_total, outer_total])[None]
    every_block = gathered_copies(stacked, "rad", 0)
    position = jnp.arange(every_block.shape[0], dtype=jnp.int32)
    own_block = lax.axis_index("rad")
    below_mask = (position < own_block).astype(jnp.float32)[:, None, None, None]
    above_mask = (position > own_block).astype(jnp.float32)[:, None, None, None]
    from_below = jnp.sum(every_block[:, 0] * below_mask, 0)
    from_above = jnp.sum(every_block[:, 1] * above_mask, 0)
    inner_sum = from_below[:, None] + jnp.cumsum(inner_terms, 1) - 0.5 * inner_terms
    outer_sum = (
        from_above[:, None]
        + jnp.flip(jnp.cumsum(jnp.flip(outer_terms, 1), 1), 1)
        - 0.5 * outer_terms
    )
    factor = (-COUPLING * 4.0 * math.pi / (2.0 * degree + 1.0))[None, None, :, None]
    coefficient = factor * (
        (radius[:, None] ** (-(degree[None, :] + 1.0)))[None, :, :, None] * inner_sum
        + (radius[:, None] ** degree[None, :])[None, :, :, None] * outer_sum
    )
    spread = jnp.einsum("frlk,tlk->frtk", coefficient, legendre, precision=lax.Precision.HIGHEST)
    potential = jnp.dot(
        spread.reshape(snapshots * shells * theta_rows, width),
        fourier.T,
        precision=lax.Precision.HIGHEST,
        preferred_element_type=jnp.float32,
    )
    return potential.reshape(snapshots, shells, theta_rows, phi_cells)


def solution(mesh):
    return jax.shard_map(
        body,
        mesh=mesh,
        in_specs=(P(None, "rad", "ang", None),),
        out_specs=P(None, "rad", "ang", None),
        check_vma=False,
    )
```

profile of v0, /device:TPU:1, one launch (start us, length us, event | category | flops | bytes accessed | tf_op | source)
XLA Modules:
  0.0 118.4 jit_solution(251214958777587090)
XLA Ops:
  0.0 0.5 add_negate_fusion
  0.5 0.6 sine_multiply_fusion
  4.1 0.6 iota_subtract_fusion
  4.7 0.6 multiply_add_fusion
  5.4 0.3 stack.76
  5.8 0.2 stack.74
  6.0 0.2 stack.72
  6.4 0.2 stack.68
  6.6 0.2 stack.66
  6.9 0.2 stack.64
  7.1 0.2 stack.62
  7.3 0.2 stack.60
  7.6 0.6 copy.46
  8.2 0.2 stack.56
  8.4 0.6 copy.44
  9.0 0.2 stack.58
  9.3 0.6 copy.45
  9.9 15.2 %convolution_bitcast_fusion = f32[6144,25]{0,1:T(8,128)S(1)} fusion(f32[6144,512]{1,0:T(8,128)} %bitcast.78, f32[25]{0:T(128)S(1)} %fusion.30, f32[512]{0:T(512)S(1)} %iota_multiply_fusion, pred[25]{0:T(512)(128)(4,1)S(1)} %get-tuple-element.17, pred[25]{0:T(512)(128)(4,1)S(1)} %get-tuple-element.18), kind=kOutput, calls=%fused_computation | convolution fusion | flops 943782400 | bytes 13199510 | tf_op jit(solution)/shard_map/dot_general | solution.py:99
  25.1 0.8 reshape.1274
  25.9 1.0 stack.80
  27.0 5.8 %convolution_bitcast_fusion.2 = f32[3,64,13,25]{1,2,0,3:T(8,128)S(1)} fusion(f32[3,64,32,25]{2,1,0,3:T(8,128)S(1)} %reshape.1274, f32[32,13,25]{0,1,2:T(8,128)S(1)} %stack.80, f32[32]{0:T(128)} %sine_multiply_fusion), kind=kOutput, calls=%fused_computation.2 | convolution fusion | flops 23972000 | bytes 905728 | tf_op jit(solution)/shard_map/frtk,tlk->frlk/dot_general | solution.py:106
  32.8 0.3 copy.52
  33.0 0.4 reshape.1275
  33.4 0.3 copy-done.6
  33.7 0.8 convolution_bitcast_fusion.3
  34.6 17.3 %all-gather.1 = f32[8,192,169]{1,2,0:T(8,128)S(1)} all-gather(f32[1,192,169]{1,2,0:T(8,128)S(1)} %convolution_bitcast_fusion.3), channel_id=2, replica_groups=mesh['rad'=16,'ang'=8] {'ang'}, dimensions={0}, use_global_device_ids=true | all-gather | bytes 1168128 | tf_op jit(solution)/shard_map/all_gather | solution.py:17
  52.3 1.7 %fusion.37 = (f32[3,13,25]{2,1,0:T(8,128)S(1)}, f32[3,64,13,25]{1,3,2,0:T(8,128)}, f32[3,13,25]{2,1,0:T(8,128)S(1)}, f32[3,64,13,25]{1,3,2,0:T(8,128)S(1)}) fusion(f32[64,13]{0,1:T(8,128)S(1)} %get-tuple-element.14, f32[64,13]{0,1:T(8,128)S(1)} %get-tuple-element.15, f32[3,64,169,1]{2,1,3,0:T(8,128)S(1)} %bitcast.81, f32[13,25,169,1]{2,1,0,3:T(8,128)S(1)} %copy-done.5), kind=kOutput, calls=%fused_computation.203 | convolution fusion | flops 126794848 | bytes 863148 | tf_op jit(solution)/shard_map/dot_general | solution.py:120
  54.1 0.2 broadcast_bitcast_fusion
  54.3 1.7 %reshape.1286 = f32[16,1,1950]{2,1,0:T(1,128)} reshape(f32[16,1,3,13,2,25]{5,4,3,2,1,0:T(2,128)S(1)} %broadcast_bitcast_fusion) | data formatting | bytes 249600
  55.9 6.8 %all-to-all-start = ((f32[16,1,1950]{2,1,0:T(1,128)}), f32[16,1,1950]{2,1,0:T(1,128)S(1)}, u32[]{:S(2)}, u32[]{:S(2)}) async-start(f32[16,1,1950]{2,1,0:T(1,128)} %reshape.1286), calls=%async_computation | async-start | bytes 262144 | tf_op jit(solution)/shard_map/all_to_all | solution.py:28
  62.7 0.8 rev.7
  63.6 0.8 copy.57
  64.3 19.7 %fusion.40 = f32[3,64,13,25]{3,2,1,0:T(8,128)S(1)} fusion(f32[3,64,13,25]{3,2,1,0:T(8,128)S(1)} %copy.57), kind=kOutput, calls=%fused_computation.207 | output fusion | flops 3931200 | bytes 499200 | tf_op jit(solution)/shard_map/jit(cumsum)/reduce_window_sum | solution.py:139
  84.0 2.9 %copy.55 = f32[3,64,13,25]{3,2,1,0:T(8,128)} copy(f32[3,64,13,25]{1,3,2,0:T(8,128)} %get-tuple-element.8) | data formatting | bytes 499200 | tf_op jit(solution)/shard_map/mul | solution.py:124
  86.8 1.5 %fusion.39 = f32[3,64,13,25]{3,2,1,0:T(8,128)S(1)} fusion(f32[3,64,13,25]{3,2,1,0:T(8,128)} %copy.55), kind=kOutput, calls=%fused_computation.206 | output fusion | flops 3931200 | bytes 499200 | tf_op jit(solution)/shard_map/jit(cumsum)/reduce_window_sum | solution.py:136
  88.4 0.6 add_divide_fusion
  88.9 1.4 %copy.58 = f32[3,64,13,25]{1,3,2,0:T(8,128)} copy(f32[3,64,13,25]{3,2,1,0:T(8,128)S(1)} %fusion.40) | data formatting | bytes 499200 | tf_op jit(solution)/shard_map/jit(cumsum)/reduce_window_sum | solution.py:139
  90.3 2.1 %rev.8 = f32[3,64,13,25]{1,3,2,0:T(8,128)} reverse(f32[3,64,13,25]{1,3,2,0:T(8,128)} %copy.58), dimensions={1} | reverse | bytes 499200 | tf_op jit(solution)/shard_map/jit(_flip)/rev | solution.py:139
  92.4 1.4 %copy.56 = f32[3,64,13,25]{1,3,2,0:T(8,128)} copy(f32[3,64,13,25]{3,2,1,0:T(8,128)S(1)} %fusion.39) | data formatting | bytes 499200 | tf_op jit(solution)/shard_map/jit(cumsum)/reduce_window_sum | solution.py:136
  93.8 0.5 compare_convert_fusion
  94.3 0.5 broadcast.6543
  94.8 1.6 %reduce.1 = f32[16,1950]{1,0:T(8,128)} reduce(f32[16,1,1950]{2,1,0:T(1,128)S(1)} %all-to-all-done, f32[]{:T(128)} %broadcast.6543), dimensions={1}, to_apply=%all_to_all.3.reduce_sub_computation | reduce | bytes 249604 | tf_op jit(solution)/shard_map/all_to_all | solution.py:28
  96.4 1.4 %reshape.1287 = f32[16,1,3,13,2,25]{5,4,3,2,1,0:T(2,128)S(1)} reshape(f32[16,1950]{1,0:T(8,128)} %reduce.1) | data formatting | bytes 249600
  97.9 0.8 fusion.4
  98.7 1.1 add_multiply_fusion
  99.8 2.5 %convolution_bitcast_fusion.1 = f32[3,64,32,25]{1,2,0,3:T(8,128)} fusion(f32[3,64,13,25]{1,3,2,0:T(8,128)S(1)} %add_multiply_fusion, f32[32,13,25]{0,1,2:T(8,128)S(1)} %stack.80), kind=kOutput, calls=%fused_computation.1 | convolution fusion | flops 23961600 | bytes 905600 | tf_op jit(solution)/shard_map/frlk,tlk->frtk/dot_general | solution.py:147
  102.3 2.9 %copy.60 = f32[3,64,32,25]{3,2,1,0:T(8,128)S(1)} copy(f32[3,64,32,25]{1,2,0,3:T(8,128)} %convolution_bitcast_fusion.1) | data formatting | bytes 1228800 | tf_op jit(solution)/shard_map/frlk,tlk->frtk/transpose | solution.py:147
  105.2 13.2 %fusion.15 = f32[3,64,32,512]{3,2,1,0:T(8,128)} fusion(f32[3,64,32,25]{3,2,1,0:T(8,128)S(1)} %copy.60, f32[25]{0:T(128)S(1)} %fusion.30, f32[512]{0:T(512)S(1)} %iota_multiply_fusion, pred[25]{0:T(512)(128)(4,1)S(1)} %copy-done.8, pred[25]{0:T(512)(128)(4,1)S(1)} %copy-done.10), kind=kOutput, calls=%fused_computation.26 | convolution fusion | flops 943782400 | bytes 13199510 | tf_op jit(solution)/shard_map/dot_general | solution.py:148
  (100 shorter events, 3.7 us)
Async XLA Ops:
  4.7 20.4 %copy-start.7 = (pred[25]{0:T(512)(128)(4,1)}, pred[25]{0:T(512)(128)(4,1)S(1)}, u32[]{:S(2)}) copy-start(pred[25]{0:T(512)(128)(4,1)S(1)} %get-tuple-element.17) | copy-start | bytes 79
  4.7 20.4 %copy-start.9 = (pred[25]{0:T(512)(128)(4,1)}, pred[25]{0:T(512)(128)(4,1)S(1)}, u32[]{:S(2)}) copy-start(pred[25]{0:T(512)(128)(4,1)S(1)} %get-tuple-element.18) | copy-start | bytes 79
  32.7 1.0 copy-start.6
  34.5 17.6 %copy-start.11 = (f32[13]{0:T(128)S(1)}, f32[13]{0:T(128)}, u32[]{:S(2)}) copy-start(f32[13]{0:T(128)} %add_negate_fusion) | copy-start | bytes 160
  34.5 17.6 %copy-start.12 = (f32[13]{0:T(128)S(1)}, f32[13]{0:T(128)}, u32[]{:S(2)}) copy-start(f32[13]{0:T(128)} %get-tuple-element.111) | copy-start | bytes 160
  34.6 17.6 %copy-start.13 = (f32[13]{0:T(128)S(1)}, f32[13]{0:T(128)}, u32[]{:S(2)}) copy-start(f32[13]{0:T(128)} %get-tuple-element.112) | copy-start | bytes 160
  34.6 17.6 %copy-start.14 = (f32[64]{0:T(128)S(1)}, f32[64]{0:T(128)}, u32[]{:S(2)}) copy-start(f32[64]{0:T(128)} %multiply_add_fusion) | copy-start | bytes 772
  34.6 17.7 %copy-start.5 = (f32[13,25,169,1]{2,1,0,3:T(8,128)S(1)}, f32[13,25,169,1]{2,1,0,3:T(8,128)}, u32[]{:S(2)}) copy-start(f32[13,25,169,1]{2,1,0,3:T(8,128)} %constant.443) | copy-start | bytes 659104
  54.0 9.6 %copy-start = (f32[3,64,13,25]{1,3,2,0:T(8,128)}, f32[3,64,13,25]{1,3,2,0:T(8,128)S(1)}, u32[]{:S(2)}) copy-start(f32[3,64,13,25]{1,3,2,0:T(8,128)S(1)} %get-tuple-element.12) | copy-start | bytes 748804
  55.9 38.4 %all-to-all-start = ((f32[16,1,1950]{2,1,0:T(1,128)}), f32[16,1,1950]{2,1,0:T(1,128)S(1)}, u32[]{:S(2)}, u32[]{:S(2)}) async-start(f32[16,1,1950]{2,1,0:T(1,128)} %reshape.1286), calls=%async_computation | async-start | bytes 262144 | tf_op jit(solution)/shard_map/all_to_all | solution.py:28
  93.8 4.9 %copy-start.1 = (f32[3,64,13,25]{1,3,2,0:T(8,128)S(1)}, f32[3,64,13,25]{1,3,2,0:T(8,128)}, u32[]{:S(2)}) copy-start(f32[3,64,13,25]{1,3,2,0:T(8,128)} %copy-done) | copy-start | bytes 748804
  93.8 4.9 %copy-start.2 = (f32[3,64,13,25]{1,3,2,0:T(8,128)S(1)}, f32[3,64,13,25]{1,3,2,0:T(8,128)}, u32[]{:S(2)}) copy-start(f32[3,64,13,25]{1,3,2,0:T(8,128)} %get-tuple-element.8) | copy-start | bytes 748804
  93.8 4.9 %copy-start.3 = (f32[3,64,13,25]{1,3,2,0:T(8,128)S(1)}, f32[3,64,13,25]{1,3,2,0:T(8,128)}, u32[]{:S(2)}) copy-start(f32[3,64,13,25]{1,3,2,0:T(8,128)} %rev.8) | copy-start | bytes 748804
  93.8 4.9 %copy-start.4 = (f32[3,64,13,25]{1,3,2,0:T(8,128)S(1)}, f32[3,64,13,25]{1,3,2,0:T(8,128)}, u32[]{:S(2)}) copy-start(f32[3,64,13,25]{1,3,2,0:T(8,128)} %copy.56) | copy-start | bytes 748804
  102.3 2.9 %copy-start.8 = (pred[25]{0:T(512)(128)(4,1)S(1)}, pred[25]{0:T(512)(128)(4,1)}, u32[]{:S(2)}) copy-start(pred[25]{0:T(512)(128)(4,1)} %copy-done.7) | copy-start | bytes 79
  102.3 2.9 %copy-start.10 = (pred[25]{0:T(512)(128)(4,1)S(1)}, pred[25]{0:T(512)(128)(4,1)}, u32[]{:S(2)}) copy-start(pred[25]{0:T(512)(128)(4,1)} %copy-done.9) | copy-start | bytes 79
where the time goes:
time: 119 us; the launch traced here: 118 us
  matrix products  39.1 us (33%)
  other arithmetic  31.1 us (26%)
  local copies, waits for them, and re-layouts  23.4 us (20%)
  blocking collectives  17.3 us (15%)
  starting transfers between devices  6.75 us (6%)
    another operation x1, other arithmetic, body(): jnp.cumsum(jnp.flip(outer_terms, 1), 1)  19.7 us
    all_gather x1, blocking collectives, over_pieces(): return lax.all_gather(value, axis).sum(0)  17.3 us
    dot_general x1, matrix products, body(): jnp.dot(density.reshape(snapshots * shells * theta_rows, phi_cells), four...  15.2 us
    dot_general x1, matrix products, body(): jnp.dot(spread.reshape(snapshots * shells * theta_rows, width), fourier.T...  13.2 us
    all_to_all x1, starting transfers between devices, from_everyone(): lax.all_to_all(jnp.broadcast_to(value[None], (count, *value.shape)), axis...  6.75 us
    dot_general x1, matrix products, body(): jnp.einsum('frtk,tlk->frlk', azimuthal, legendre * weights[:, None, None]...  5.79 us
    unnamed x33, local copies, waits for them, and re-layouts  3.63 us
    another operation x13, local copies, waits for them, and re-layouts, legendre_table(): return jnp.stack(degree_rows, 1)  2.96 us
  transfers between devices with their start and end apart: 1, of which 0 were waited for; matrix products, arithmetic and copies ran while one was open for 27% of the time, Pallas kernels for 0%

commit v1 on v0

v1 whole, which is shorter than its diff:
```python
import functools
import math

import jax
import jax.numpy as jnp
import numpy as np
from jax import lax
from jax.experimental import pallas as pl
from jax.experimental.pallas import tpu as pltpu
from jax.sharding import PartitionSpec as P

LMAX = 12
NPHI = 512
NTH = 256
NR = 1024
FIELDS = 3
HALF = NPHI // 2
INNER = 0.5
COUPLING = 2000.0
MESH = pl.DeviceIdType.MESH
F32 = jnp.float32
BF16 = jnp.bfloat16
LANES = 128

SHELLS = 64
ROWS = 32
NRAD = 16
NANG = 8
GROUP = SHELLS // NANG
STEP = 16
OUT_STEP = 16


def slots(parity):
    return [
        (l, k)
        for l in range(LMAX + 1)
        for k in range(2 * LMAX + 1)
        if (k + 1) // 2 <= l and ((k + 1) // 2) % 2 == parity
    ]


def legendre():
    theta = (np.arange(NTH) + 0.5) * (math.pi / NTH)
    c, s = np.cos(theta), np.sin(theta)
    v = {(0, 0): np.full_like(theta, 1.0 / math.sqrt(4.0 * math.pi))}
    for m in range(1, LMAX + 1):
        v[m, m] = math.sqrt((2.0 * m + 1.0) / (2.0 * m)) * s * v[m - 1, m - 1]
    for m in range(LMAX):
        v[m + 1, m] = math.sqrt(2.0 * m + 3.0) * c * v[m, m]
    for m in range(LMAX + 1):
        for l in range(m + 2, LMAX + 1):
            a = math.sqrt((4.0 * l * l - 1.0) / (l * l - m * m))
            b = math.sqrt(((l - 1.0) ** 2 - m * m) / (4.0 * (l - 1.0) ** 2 - 1.0))
            v[l, m] = a * (c * v[l - 1, m] - b * v[l - 2, m])
    weight = s * (math.pi / NTH) * (2.0 * math.pi / NPHI)
    return v, weight


def fourier():
    phi = np.arange(NPHI) * (2.0 * math.pi / NPHI)
    columns = [np.ones_like(phi)]
    for m in range(1, LMAX + 1):
        columns.append(math.sqrt(2.0) * np.cos(m * phi))
        columns.append(math.sqrt(2.0) * np.sin(m * phi))
    return columns


def hi_lo(table):
    hi = table.astype(np.float32).astype(BF16)
    lo = (table - hi.astype(np.float64)).astype(np.float32).astype(BF16)
    return hi, lo


def tables():
    v, weight = legendre()
    columns = fourier()
    forward = np.zeros((2, HALF, 2 * LANES), BF16)
    backward = np.zeros((2, 2 * LANES, HALF), BF16)
    moment = np.zeros((NTH, 2 * LANES), np.float32)
    spread = np.zeros((NTH, 4 * LANES), np.float32)
    misc = np.zeros((8, 2 * LANES), np.float32)
    misc[1] = 0.0
    for parity in range(2):
        used = slots(parity)
        n = len(used)
        f = np.stack([columns[k][:HALF] for _, k in used], -1)
        hi, lo = hi_lo(f)
        forward[parity, :, :n] = hi
        forward[parity, :, LANES : LANES + n] = lo
        backward[parity, :n] = hi.T
        backward[parity, 85 : 85 + n] = hi.T
        backward[parity, 170 : 170 + n] = lo.T
        table = np.stack([v[l, (k + 1) // 2] for l, k in used], -1)
        at = parity * LANES
        moment[:, at : at + n] = table * weight[:, None]
        for copy in range(3):
            start = 2 * at + 85 * copy
            spread[:, start : start + n] = table
        degree = np.array([l for l, _ in used], np.float64)
        misc[0, at : at + n] = degree
        misc[1, at : at + n] = -COUPLING * 4.0 * math.pi / (2.0 * degree + 1.0)
    return forward, backward, moment, spread, misc


def analyse(
    dens,
    forward,
    moment,
    misc,
    out,
    held,
    fwd,
    mom,
    mis,
    radial,
    part,
    got,
    mine,
    whole,
    tot_out,
    tot_in,
    car_out,
    car_in,
    dens_sem,
    tab_sem,
    rs_send,
    rs_recv,
    ag_send,
    ag_recv,
    tot_send,
    tot_recv,
    car_send,
    car_recv,
):
    me_r = lax.axis_index("rad")
    me_a = lax.axis_index("ang")
    steps = SHELLS // STEP

    def density_copy(f, c):
        at = pl.ds(c * STEP, STEP)
        return pltpu.make_async_copy(
            dens.at[f, at], held.at[f, at], dens_sem.at[f * steps + c]
        )

    first = pltpu.make_async_copy(forward, fwd, tab_sem.at[0])
    second = pltpu.make_async_copy(
        moment.at[pl.ds(pl.multiple_of(me_a * ROWS, ROWS), ROWS)], mom, tab_sem.at[1]
    )
    third = pltpu.make_async_copy(misc, mis, tab_sem.at[2])
    first.start()
    second.start()
    third.start()
    for f in range(FIELDS):
        for c in range(steps):
            density_copy(f, c).start()

    barrier = pltpu.get_barrier_semaphore()
    for d in range(1, NANG):
        pl.semaphore_signal(
            barrier,
            inc=1,
            device_id=(me_r, lax.rem(me_a + d, NANG)),
            device_id_type=MESH,
        )
    for d in range(1, NRAD):
        pl.semaphore_signal(
            barrier,
            inc=1,
            device_id=(lax.rem(me_r + d, NRAD), me_a),
            device_id_type=MESH,
        )

    third.wait()
    shell = lax.broadcasted_iota(jnp.int32, (SHELLS, 2 * LANES), 0) + me_r * SHELLS
    spacing = (1.0 - INNER) / NR
    radius = INNER + (shell.astype(F32) + 0.5) * spacing
    degree = mis[0:1, :]
    factor = mis[1:2, :]
    power = jnp.exp(degree * jnp.log(radius))
    inverse = 1.0 / power
    radial[0] = power * radius * radius * spacing
    radial[1] = inverse * radius * spacing
    radial[2] = factor * inverse / radius
    radial[3] = factor * power
    tot_in[me_r] = jnp.zeros((4, 2 * LANES), F32)
    tot_out[...] = jnp.zeros((2, 4, 2 * LANES), F32)
    first.wait()
    second.wait()
    pl.semaphore_wait(barrier, NANG + NRAD - 2)

    def rs_copy(f, d):
        peer = lax.rem(me_a + d, NANG)
        return pltpu.make_async_remote_copy(
            src_ref=part.at[f, peer],
            dst_ref=got.at[f, me_a],
            send_sem=rs_send.at[f, d],
            recv_sem=rs_recv.at[f, me_a],
            device_id=(me_r, peer),
            device_id_type=MESH,
        )

    def rs_arrival(f, d):
        source = lax.rem(me_a + d, NANG)
        return pltpu.make_async_remote_copy(
            src_ref=part.at[f, source],
            dst_ref=got.at[f, source],
            send_sem=rs_send.at[f, d],
            recv_sem=rs_recv.at[f, source],
            device_id=(me_r, source),
            device_id_type=MESH,
        )

    def ag_copy(f, d):
        peer = lax.rem(me_a + d, NANG)
        return pltpu.make_async_remote_copy(
            src_ref=mine.at[f],
            dst_ref=whole.at[f, me_a],
            send_sem=ag_send.at[f, d],
            recv_sem=ag_recv.at[f, me_a],
            device_id=(me_r, peer),
            device_id_type=MESH,
        )

    def ag_arrival(f, d):
        source = lax.rem(me_a + d, NANG)
        return pltpu.make_async_remote_copy(
            src_ref=mine.at[f],
            dst_ref=whole.at[f, source],
            send_sem=ag_send.at[f, d],
            recv_sem=ag_recv.at[f, source],
            device_id=(me_r, source),
            device_id_type=MESH,
        )

    def tot_copy(d):
        peer = lax.rem(me_r + d, NRAD)
        return pltpu.make_async_remote_copy(
            src_ref=tot_out.at[lax.div(me_r + d, NRAD)],
            dst_ref=tot_in.at[me_r],
            send_sem=tot_send.at[d],
            recv_sem=tot_recv.at[me_r],
            device_id=(peer, me_a),
            device_id_type=MESH,
        )

    def tot_arrival(d):
        source = lax.rem(me_r + d, NRAD)
        return pltpu.make_async_remote_copy(
            src_ref=tot_out.at[0],
            dst_ref=tot_in.at[source],
            send_sem=tot_send.at[d],
            recv_sem=tot_recv.at[source],
            device_id=(source, me_a),
            device_id_type=MESH,
        )

    def car_copy(d):
        peer = lax.rem(me_a + d, NANG)
        return pltpu.make_async_remote_copy(
            src_ref=car_out,
            dst_ref=car_in.at[me_a],
            send_sem=car_send.at[d],
            recv_sem=car_recv.at[me_a],
            device_id=(me_r, peer),
            device_id_type=MESH,
        )

    def car_arrival(d):
        source = lax.rem(me_a + d, NANG)
        return pltpu.make_async_remote_copy(
            src_ref=car_out,
            dst_ref=car_in.at[source],
            send_sem=car_send.at[d],
            recv_sem=car_recv.at[source],
            device_id=(me_r, source),
            device_id_type=MESH,
        )

    def snapshot(f, _):
        def chunk(c, _):
            density_copy(f, c).wait()
            x = held[f, pl.ds(c * STEP, STEP)].reshape(STEP * ROWS, NPHI)
            left, right = x[:, :HALF], x[:, HALF:]
            sums = []
            for parity in range(2):
                y = left + right if parity == 0 else left - right
                hi = y.astype(BF16)
                lo = (y - hi.astype(F32)).astype(BF16)
                weights = fwd[parity]
                p = jnp.dot(hi, weights, preferred_element_type=F32) + jnp.dot(
                    lo, weights, preferred_element_type=F32
                )
                a = (p[:, :LANES] + p[:, LANES:]).reshape(STEP, ROWS, LANES)
                w = mom[:, parity * LANES : (parity + 1) * LANES]
                sums.append(jnp.sum(a * w[None], 1))
            both = jnp.concatenate(sums, -1)
            part[f, pl.ds(c * (STEP // GROUP), STEP // GROUP)] = both.reshape(
                STEP // GROUP, GROUP, 2 * LANES
            )
            return 0

        lax.fori_loop(0, steps, chunk, 0)
        for d in range(1, NANG):
            rs_copy(f, d).start()
        moments = part[f].reshape(SHELLS, 2 * LANES)
        for side in range(2):
            tot_out[side, pl.ds(f, 1)] = jnp.sum(moments * radial[side], 0, keepdims=True)
        return 0

    lax.fori_loop(0, FIELDS, snapshot, 0)
    for d in range(1, NRAD):
        tot_copy(d).start()

    def reduce(f, _):
        total = part[f, me_a]
        for d in range(1, NANG):
            rs_arrival(f, d).wait_recv()
            total += got[f, lax.rem(me_a + d, NANG)]
        mine[f] = total
        whole[f, me_a] = total
        for d in range(1, NANG):
            ag_copy(f, d).start()
        return 0

    lax.fori_loop(0, FIELDS, reduce, 0)

    for d in range(1, NRAD):
        tot_arrival(d).wait_recv()
    below = jnp.zeros((4, 2 * LANES), F32)
    above = jnp.zeros((4, 2 * LANES), F32)
    for r in range(NRAD):
        term = tot_in[r]
        below += jnp.where(r < me_r, term, 0.0)
        above += jnp.where(r > me_r, term, 0.0)
    car_out[0] = below
    car_out[1] = above
    car_in[me_a, 0] = below
    car_in[me_a, 1] = above
    for d in range(1, NANG):
        car_copy(d).start()

    row = lax.broadcasted_iota(jnp.int32, (SHELLS, SHELLS), 0)
    col = lax.broadcasted_iota(jnp.int32, (SHELLS, SHELLS), 1)
    same = jnp.where(row == col, 0.5, 0.0)
    lower = (jnp.where(col < row, 1.0, 0.0) + same).astype(BF16)
    upper = (jnp.where(col > row, 1.0, 0.0) + same).astype(BF16)

    def running(triangle, terms):
        hi = terms.astype(BF16)
        rest = terms - hi.astype(F32)
        mid = rest.astype(BF16)
        lo = (rest - mid.astype(F32)).astype(BF16)
        total = jnp.dot(triangle, hi, preferred_element_type=F32)
        total += jnp.dot(triangle, mid, preferred_element_type=F32)
        return total + jnp.dot(triangle, lo, preferred_element_type=F32)

    def tripled(half):
        zeros = jnp.zeros((SHELLS, LANES), F32)
        wide = jnp.concatenate([half, zeros], -1)
        return wide + pltpu.roll(wide, 85, 1) + pltpu.roll(wide, 170, 1)

    def put(f, value):
        for parity in range(2):
            out[pl.ds(pl.multiple_of(f * SHELLS, SHELLS), SHELLS), pl.ds(parity * 2 * LANES, 2 * LANES)] = (
                tripled(value[:, parity * LANES : (parity + 1) * LANES])
            )

    for f in range(FIELDS):
        for d in range(1, NANG):
            ag_arrival(f, d).wait_recv()
        moments = whole[f].reshape(SHELLS, 2 * LANES)
        inner = running(lower, moments * radial[0])
        outer = running(upper, moments * radial[1])
        if f == 0:
            for d in range(1, NANG):
                car_arrival(d).wait_recv()
            carry = car_in[0]
            for a in range(1, NANG):
                carry += car_in[a]
        inner += carry[0, f : f + 1]
        outer += carry[1, f : f + 1]
        put(f, radial[2] * inner + radial[3] * outer)

    for f in range(FIELDS):
        for d in range(1, NANG):
            rs_copy(f, d).wait_send()
            ag_copy(f, d).wait_send()
    for d in range(1, NANG):
        car_copy(d).wait_send()
    for d in range(1, NRAD):
        tot_copy(d).wait_send()


def synthesise(coef, bwd, spread, out, held, out_sem):
    own = pl.ds(pl.multiple_of(lax.axis_index("ang") * ROWS, ROWS), ROWS)
    steps = FIELDS * SHELLS // OUT_STEP

    def out_copy(c):
        at = pl.ds(c * OUT_STEP, OUT_STEP)
        return pltpu.make_async_copy(held.at[at], out.at[at], out_sem.at[c])

    lane = lax.broadcasted_iota(jnp.int32, (OUT_STEP * ROWS, 2 * LANES), 1)
    keep = jnp.logical_and(lane >= 85, lane < 170)

    def chunk(c, _):
        z = []
        for parity in range(2):
            at = pl.ds(parity * 2 * LANES, 2 * LANES)
            row = coef[pl.ds(pl.multiple_of(c * OUT_STEP, OUT_STEP), OUT_STEP), at]
            x = (row[:, None, :] * spread[own, at][None]).reshape(OUT_STEP * ROWS, 2 * LANES)
            hi = x.astype(BF16).astype(F32)
            z.append(
                jnp.dot(
                    jnp.where(keep, x - hi, hi).astype(BF16),
                    bwd[parity],
                    preferred_element_type=F32,
                )
            )
        both = jnp.concatenate([z[0] + z[1], z[0] - z[1]], -1)
        held[pl.ds(c * OUT_STEP, OUT_STEP)] = both.reshape(OUT_STEP, ROWS, NPHI)
        out_copy(c).start()
        return 0

    lax.fori_loop(0, steps, chunk, 0)
    for c in range(steps):
        out_copy(c).wait()


def body(density):
    forward, backward, moment, spread, misc = tables()
    hbm = pl.BlockSpec(memory_space=pltpu.HBM)
    vmem = pl.BlockSpec(memory_space=pltpu.VMEM)
    dma = pltpu.SemaphoreType.DMA
    wide = 2 * LANES
    coef = pl.pallas_call(
        analyse,
        out_shape=jax.ShapeDtypeStruct((FIELDS * SHELLS, 4 * LANES), F32),
        in_specs=[hbm] * 4,
        out_specs=vmem,
        scratch_shapes=[
            pltpu.VMEM((FIELDS, SHELLS, ROWS, NPHI), F32),
            pltpu.VMEM((2, HALF, wide), BF16),
            pltpu.VMEM((ROWS, wide), F32),
            pltpu.VMEM((8, wide), F32),
            pltpu.VMEM((4, SHELLS, wide), F32),
            pltpu.VMEM((FIELDS, NANG, GROUP, wide), F32),
            pltpu.VMEM((FIELDS, NANG, GROUP, wide), F32),
            pltpu.VMEM((FIELDS, GROUP, wide), F32),
            pltpu.VMEM((FIELDS, NANG, GROUP, wide), F32),
            pltpu.VMEM((2, 4, wide), F32),
            pltpu.VMEM((NRAD, 4, wide), F32),
            pltpu.VMEM((2, 4, wide), F32),
            pltpu.VMEM((NANG, 2, 4, wide), F32),
            dma((FIELDS * SHELLS // STEP,)),
            dma((3,)),
            dma((FIELDS, NANG)),
            dma((FIELDS, NANG)),
            dma((FIELDS, NANG)),
            dma((FIELDS, NANG)),
            dma((NRAD,)),
            dma((NRAD,)),
            dma((NANG,)),
            dma((NANG,)),
        ],
        compiler_params=pltpu.CompilerParams(
            collective_id=0, has_side_effects=True, vmem_limit_bytes=40 << 20
        ),
        name="analyse",
    )(*[pltpu.with_memory_space_constraint(x, pltpu.HBM) for x in (density, jnp.asarray(forward), jnp.asarray(moment), jnp.asarray(misc))])
    potential = pl.pallas_call(
        synthesise,
        out_shape=jax.ShapeDtypeStruct((FIELDS * SHELLS, ROWS, NPHI), F32),
        in_specs=[vmem, vmem, vmem],
        out_specs=hbm,
        scratch_shapes=[
            pltpu.VMEM((FIELDS * SHELLS, ROWS, NPHI), F32),
            dma((FIELDS * SHELLS // OUT_STEP,)),
        ],
        compiler_params=pltpu.CompilerParams(vmem_limit_bytes=40 << 20),
        name="synthesise",
    )(coef, jnp.asarray(backward), jnp.asarray(spread))
    return potential.reshape(FIELDS, SHELLS, ROWS, NPHI)


def solution(mesh):
    return jax.shard_map(
        body,
        mesh=mesh,
        in_specs=(P(None, "rad", "ang", None),),
        out_specs=P(None, "rad", "ang", None),
        check_vma=False,
    )
```

time: 119 us -> 31.9 us (0.27)
  matrix products: 39.1 us -> 0 us
  Pallas kernels: 0 us -> 31.8 us
  other arithmetic: 31.1 us -> 0 us
  local copies, waits for them, and re-layouts: 23.4 us -> 0.01 us
  blocking collectives: 17.3 us -> 0 us
  starting transfers between devices: 6.75 us -> 0 us
    dot_general x6 -> x0, matrix products: 39.1 us -> none  [the longest x1 15.2 us: body(): jnp.dot(density.reshape(snapshots * shells * theta_rows, phi_cells), four...]
    pallas_call x0 -> x2, Pallas kernels: none -> 31.8 us  [the longest x1 26.4 us: body(): pl.pallas_call(analyse, out_shape=jax.ShapeDtypeStruct((FIELDS * SHELLS,...]
    another operation x3 -> x0, other arithmetic: 21.2 us -> none  [the longest x1 19.7 us: body(): jnp.cumsum(jnp.flip(outer_terms, 1), 1)]
    all_gather x1 -> x0, blocking collectives: 17.3 us -> none  [over_pieces(): return lax.all_gather(value, axis).sum(0)]
    another operation x33 -> x0, local copies, waits for them, and re-layouts: 8.21 us -> none  [the longest x13 2.96 us: legendre_table(): return jnp.stack(degree_rows, 1)]
    all_to_all x1 -> x0, starting transfers between devices: 6.75 us -> none  [from_everyone(): lax.all_to_all(jnp.broadcast_to(value[None], (count, *value.shape)), axis...]
    mul x48 -> x0, other arithmetic: 4.56 us -> none  [the longest x33 2.22 us: legendre_table(): coef_a * (cos_theta * values_lm[l - 1, m] - coef_b * values_lm[l - 2, m])]
    rev x3 -> x0, local copies, waits for them, and re-layouts: 3.69 us -> none  [the longest x1 2.09 us: body(): jnp.flip(jnp.cumsum(jnp.flip(outer_terms, 1), 1), 1)]
  transfers between devices with their start and end apart: 1 -> 0, of which waited for: 0 -> 0; matrix products, arithmetic and copies ran while one was open for 27% -> 0% of each run, Pallas kernels for 0% -> 0%
where the time goes in v1:
time: 31.9 us; the launch traced here: 31.8 us
  Pallas kernels  31.8 us (100%)
    pallas_call x1, Pallas kernels, body(): pl.pallas_call(analyse, out_shape=jax.ShapeDtypeStruct((FIELDS * SHELLS,...  26.4 us
    pallas_call x1, Pallas kernels, body(): pl.pallas_call(synthesise, out_shape=jax.ShapeDtypeStruct((FIELDS * SHELL...  5.37 us

profile of v1, /device:TPU:1, one launch (start us, length us, event | category | flops | bytes accessed | tf_op | source)
XLA Modules:
  0.0 31.8 jit_solution(5107587869251629269)
XLA Ops:
  0.0 0.0 copy-start
  0.0 0.0 copy-start.1
  0.0 26.4 %analyse.1.coef = f32[192,512]{1,0:T(8,128)S(1)} custom-call(f32[3,64,32,512]{3,2,1,0:T(8,128)} %dens.1, bf16[2,256,256]{2,1,0:T(8,128)(2,1)} %constant.10.clone.forward, f32[256,256]{1,0:T(8,128)} %constant.11.clone.moment, f32[8,256]{1,0:T(8,128)} %constant.12.clone.misc), custom_call_target="tpu_custom_call" | custom-call | tf_op jit(solution)/shard_map/analyse/pallas_call | solution.py:436
  26.4 0.0 copy-done
  26.4 0.0 copy-done.1
  26.4 5.4 %synthesise.1 = f32[192,32,512]{2,1,0:T(8,128)} custom-call(f32[192,512]{1,0:T(8,128)S(1)} %analyse.1.coef, bf16[2,256,256]{2,1,0:T(8,128)(2,1)S(1)} %copy-done.1, f32[256,512]{1,0:T(8,128)S(1)} %copy-done), custom_call_target="tpu_custom_call" | custom-call | tf_op jit(solution)/shard_map/synthesise/pallas_call | solution.py:471
Async XLA Ops:
  0.0 26.4 %copy-start = (f32[256,512]{1,0:T(8,128)S(1)}, f32[256,512]{1,0:T(8,128)}, u32[]{:S(2)}) copy-start(f32[256,512]{1,0:T(8,128)} %constant.14.clone.spread) | copy-start | bytes 1572868
  0.0 26.4 %copy-start.1 = (bf16[2,256,256]{2,1,0:T(8,128)(2,1)S(1)}, bf16[2,256,256]{2,1,0:T(8,128)(2,1)}, u32[]{:S(2)}) copy-start(bf16[2,256,256]{2,1,0:T(8,128)(2,1)} %constant.13.clone.bwd) | copy-start | bytes 786436

commit v2 on v1

v2 whole, which is shorter than its diff:
```python
import functools
import math

import jax
import jax.numpy as jnp
import numpy as np
from jax import lax
from jax.experimental import pallas as pl
from jax.experimental.pallas import tpu as pltpu
from jax.sharding import PartitionSpec as P

LMAX = 12
NPHI = 512
NTH = 256
NR = 1024
FIELDS = 3
HALF = NPHI // 2
INNER = 0.5
COUPLING = 2000.0
MESH = pl.DeviceIdType.MESH
F32 = jnp.float32
BF16 = jnp.bfloat16
LANES = 128

SHELLS = 64
ROWS = 32
NRAD = 16
NANG = 8
GROUP = SHELLS // NANG
STEP = 32
AHEAD = 2
OUT_STEP = 16
SPLIT = 85


def slots(parity):
    return [
        (l, k)
        for l in range(LMAX + 1)
        for k in range(2 * LMAX + 1)
        if (k + 1) // 2 <= l and ((k + 1) // 2) % 2 == parity
    ]


def legendre():
    theta = (np.arange(NTH) + 0.5) * (math.pi / NTH)
    c, s = np.cos(theta), np.sin(theta)
    v = {(0, 0): np.full_like(theta, 1.0 / math.sqrt(4.0 * math.pi))}
    for m in range(1, LMAX + 1):
        v[m, m] = math.sqrt((2.0 * m + 1.0) / (2.0 * m)) * s * v[m - 1, m - 1]
    for m in range(LMAX):
        v[m + 1, m] = math.sqrt(2.0 * m + 3.0) * c * v[m, m]
    for m in range(LMAX + 1):
        for l in range(m + 2, LMAX + 1):
            a = math.sqrt((4.0 * l * l - 1.0) / (l * l - m * m))
            b = math.sqrt(((l - 1.0) ** 2 - m * m) / (4.0 * (l - 1.0) ** 2 - 1.0))
            v[l, m] = a * (c * v[l - 1, m] - b * v[l - 2, m])
    weight = s * (math.pi / NTH) * (2.0 * math.pi / NPHI)
    return v, weight


def fourier():
    phi = np.arange(NPHI) * (2.0 * math.pi / NPHI)
    columns = [np.ones_like(phi)]
    for m in range(1, LMAX + 1):
        columns.append(math.sqrt(2.0) * np.cos(m * phi))
        columns.append(math.sqrt(2.0) * np.sin(m * phi))
    return columns


def hi_lo(table):
    hi = table.astype(np.float32).astype(BF16)
    lo = (table - hi.astype(np.float64)).astype(np.float32).astype(BF16)
    return hi, lo


def tables():
    v, weight = legendre()
    columns = fourier()
    forward = np.zeros((2, HALF, 2 * LANES), BF16)
    backward = np.zeros((2, 2 * LANES, HALF), BF16)
    moment = np.zeros((NTH, 2 * LANES), np.float32)
    spread = np.zeros((NTH, 4 * LANES), np.float32)
    misc = np.zeros((8, 2 * LANES), np.float32)
    rest = LANES - SPLIT
    for parity in range(2):
        used = slots(parity)
        n = len(used)
        f = np.stack([columns[k][:HALF] for _, k in used], -1)
        hi, lo = hi_lo(f)
        forward[parity, :, :n] = hi
        forward[parity, :, LANES : LANES + n] = lo
        table = np.stack([v[l, (k + 1) // 2] for l, k in used], -1)
        at = parity * LANES
        moment[:, at : at + n] = table * weight[:, None]
        for half in range(2):
            row = half * LANES
            backward[parity, row : row + n] = hi.T
            part = slice(0, rest) if half == 0 else slice(rest, n)
            size = part.stop - part.start
            backward[parity, row + SPLIT : row + SPLIT + size] = lo.T[part]
            lane = 2 * at + row
            spread[:, lane : lane + n] = table
            spread[:, lane + SPLIT : lane + SPLIT + size] = table[:, part]
        degree = np.array([l for l, _ in used], np.float64)
        misc[0, at : at + n] = degree
        misc[1, at : at + n] = -COUPLING * 4.0 * math.pi / (2.0 * degree + 1.0)
    local = np.concatenate(
        [
            moment.reshape(NANG, ROWS, 2 * LANES),
            np.broadcast_to(misc, (NANG, 8, 2 * LANES)),
        ],
        1,
    )
    return forward, backward, local, spread


def widened(value):
    lane = lax.broadcasted_iota(jnp.int32, (value.shape[0], LANES), 1)
    pieces = []
    for parity in range(2):
        half = value[:, parity * LANES : (parity + 1) * LANES]
        pieces.append(jnp.where(lane < SPLIT, half, pltpu.roll(half, SPLIT, 1)))
        pieces.append(jnp.where(lane < SPLIT, half, pltpu.roll(half, 2 * SPLIT - LANES, 1)))
    return jnp.concatenate(pieces, -1)


def analyse(
    dens,
    forward,
    local,
    out,
    held,
    fwd,
    loc,
    radial,
    radial_wide,
    part,
    got,
    mine,
    whole,
    base,
    tot_out,
    tot_in,
    car_out,
    car_in,
    dens_sem,
    tab_sem,
    rs_recv,
    ag_recv,
    tot_recv,
    car_recv,
    send_sem,
):
    me_r = lax.axis_index("rad")
    me_a = lax.axis_index("ang")
    steps = SHELLS // STEP
    total_steps = FIELDS * steps
    others = pl.ds(0, NANG - 1)

    def density_copy(g):
        f, c = lax.div(g, steps), lax.rem(g, steps)
        at = pl.ds(c * STEP, STEP)
        return pltpu.make_async_copy(
            dens.at[f, at], held.at[f, at], dens_sem.at[lax.rem(g, AHEAD + 1)]
        )

    second = pltpu.make_async_copy(local.at[me_a], loc, tab_sem.at[0])
    first = pltpu.make_async_copy(forward, fwd, tab_sem.at[1])
    second.start()
    first.start()
    for g in range(AHEAD):
        density_copy(jnp.int32(g)).start()

    barrier = pltpu.get_barrier_semaphore()
    for d in range(1, NANG):
        pl.semaphore_signal(
            barrier,
            inc=1,
            device_id=(me_r, lax.rem(me_a + d, NANG)),
            device_id_type=MESH,
        )
    for d in range(1, NRAD):
        pl.semaphore_signal(
            barrier,
            inc=1,
            device_id=(lax.rem(me_r + d, NRAD), me_a),
            device_id_type=MESH,
        )

    def send(src, dst, k, recv, rad, ang):
        return pltpu.make_async_remote_copy(
            src_ref=src,
            dst_ref=dst,
            send_sem=send_sem.at[k],
            recv_sem=recv,
            device_id=(rad, ang),
            device_id_type=MESH,
        )

    def ang_peer(d):
        return lax.rem(me_a + d, NANG)

    def rad_peer(d):
        return lax.rem(me_r + d, NRAD)

    shell = lax.broadcasted_iota(jnp.int32, (SHELLS, 2 * LANES), 0) + me_r * SHELLS
    spacing = (1.0 - INNER) / NR
    radius = INNER + (shell.astype(F32) + 0.5) * spacing
    log_radius = jnp.log(radius)
    tot_in[me_r] = jnp.zeros((4, 2 * LANES), F32)
    tot_out[...] = jnp.zeros((2, 4, 2 * LANES), F32)
    second.wait()
    degree = loc[ROWS : ROWS + 1, :]
    factor = loc[ROWS + 1 : ROWS + 2, :]
    power = jnp.exp(degree * log_radius)
    inverse = 1.0 / power
    radial[0] = power * radius * radius * spacing
    radial[1] = inverse * radius * spacing
    below_weight = factor * inverse / radius
    above_weight = factor * power
    radial[2] = below_weight
    radial[3] = above_weight
    radial_wide[0] = widened(below_weight)
    radial_wide[1] = widened(above_weight)
    first.wait()

    def snapshot(f, _):
        def chunk(c, _):
            g = f * steps + c
            density_copy(g).wait()

            @pl.when(g + AHEAD < total_steps)
            def _():
                density_copy(g + AHEAD).start()

            x = held[f, pl.ds(c * STEP, STEP)].reshape(STEP * ROWS, NPHI)
            left, right = x[:, :HALF], x[:, HALF:]
            sums = []
            for parity in range(2):
                y = left + right if parity == 0 else left - right
                hi = y.astype(BF16)
                lo = (y - hi.astype(F32)).astype(BF16)
                weights = fwd[parity]
                p = jnp.dot(hi, weights, preferred_element_type=F32) + jnp.dot(
                    lo, weights, preferred_element_type=F32
                )
                a = (p[:, :LANES] + p[:, LANES:]).reshape(STEP, ROWS, LANES)
                w = loc[:ROWS, parity * LANES : (parity + 1) * LANES]
                sums.append(jnp.sum(a * w[None], 1))
            both = jnp.concatenate(sums, -1)
            part[f, pl.ds(c * (STEP // GROUP), STEP // GROUP)] = both.reshape(
                STEP // GROUP, GROUP, 2 * LANES
            )
            return 0

        lax.fori_loop(0, steps, chunk, 0)
        moments = part[f].reshape(SHELLS, 2 * LANES)
        for side in range(2):
            tot_out[side, pl.ds(f, 1)] = jnp.sum(moments * radial[side], 0, keepdims=True)

        @pl.when(f == 0)
        def _():
            pl.semaphore_wait(barrier, NANG + NRAD - 2)

        @pl.when(f == FIELDS - 1)
        def _():
            for d in range(1, NRAD):
                send(
                    tot_out.at[lax.div(me_r + d, NRAD)],
                    tot_in.at[me_r],
                    2,
                    tot_recv.at[0],
                    rad_peer(d),
                    me_a,
                ).start()

        for d in range(1, NANG):
            send(
                part.at[f, ang_peer(d)], got.at[f, me_a], 0, rs_recv.at[f], me_r, ang_peer(d)
            ).start()
        got[f, me_a] = part[f, me_a]
        return 0

    lax.fori_loop(0, FIELDS, snapshot, 0)

    def reduce(f, _):
        send(
            part.at[f, others], got.at[f, others], 0, rs_recv.at[f], me_r, ang_peer(1)
        ).wait_recv()
        total = jnp.sum(got[f], 0)
        mine[f] = total
        whole[f, me_a] = total
        for d in range(1, NANG):
            send(
                mine.at[f], whole.at[f, me_a], 1, ag_recv.at[f], me_r, ang_peer(d)
            ).start()
        return 0

    lax.fori_loop(0, FIELDS, reduce, 0)

    arrived = pl.ds(0, NRAD - 1)
    send(
        tot_in.at[arrived], tot_in.at[arrived], 2, tot_recv.at[0], rad_peer(1), me_a
    ).wait_recv()
    below = jnp.zeros((4, 2 * LANES), F32)
    above = jnp.zeros((4, 2 * LANES), F32)
    for r in range(NRAD):
        term = tot_in[r]
        below += jnp.where(r < me_r, term, 0.0)
        above += jnp.where(r > me_r, term, 0.0)
    car_out[0] = below
    car_out[1] = above
    for d in range(1, NANG):
        send(car_out, car_in.at[me_a], 3, car_recv.at[0], me_r, ang_peer(d)).start()
    car_in[me_a, 0] = below
    car_in[me_a, 1] = above

    row = lax.broadcasted_iota(jnp.int32, (SHELLS, SHELLS), 0)
    col = lax.broadcasted_iota(jnp.int32, (SHELLS, SHELLS), 1)
    same = jnp.where(row == col, 0.5, 0.0)
    lower = (jnp.where(col < row, 1.0, 0.0) + same).astype(BF16)
    upper = (jnp.where(col > row, 1.0, 0.0) + same).astype(BF16)

    def running(triangle, terms):
        hi = terms.astype(BF16)
        rest = terms - hi.astype(F32)
        mid = rest.astype(BF16)
        lo = (rest - mid.astype(F32)).astype(BF16)
        total = jnp.dot(triangle, hi, preferred_element_type=F32)
        total += jnp.dot(triangle, mid, preferred_element_type=F32)
        return total + jnp.dot(triangle, lo, preferred_element_type=F32)

    def local_sums(f, _):
        send(
            whole.at[f, others], whole.at[f, others], 1, ag_recv.at[f], me_r, ang_peer(1)
        ).wait_recv()
        moments = whole[f].reshape(SHELLS, 2 * LANES)
        inner = running(lower, moments * radial[0])
        outer = running(upper, moments * radial[1])
        base[f] = widened(radial[2] * inner + radial[3] * outer)
        return 0

    lax.fori_loop(0, FIELDS, local_sums, 0)
    send(car_in.at[others], car_in.at[others], 3, car_recv.at[0], me_r, ang_peer(1)).wait_recv()
    carry = car_in[0]
    for a in range(1, NANG):
        carry += car_in[a]
    below = widened(carry[0])
    above = widened(carry[1])
    for f in range(FIELDS):
        out[f * SHELLS : (f + 1) * SHELLS] = (
            base[f] + radial_wide[0] * below[f : f + 1] + radial_wide[1] * above[f : f + 1]
        )

    send(
        part.at[:, others], got.at[:, others], 0, rs_recv.at[0], me_r, ang_peer(1)
    ).wait_send()
    send(
        whole.at[:, others], whole.at[:, others], 1, rs_recv.at[0], me_r, ang_peer(1)
    ).wait_send()
    send(
        tot_in.at[arrived], tot_in.at[arrived], 2, tot_recv.at[0], rad_peer(1), me_a
    ).wait_send()
    send(car_in.at[others], car_in.at[others], 3, car_recv.at[0], me_r, ang_peer(1)).wait_send()


def synthesise(coef, bwd, spread, out, held, out_sem):
    own = pl.ds(pl.multiple_of(lax.axis_index("ang") * ROWS, ROWS), ROWS)
    steps = FIELDS * SHELLS // OUT_STEP
    lane = lax.broadcasted_iota(jnp.int32, (OUT_STEP * ROWS, LANES), 1)

    def chunk(c, _):
        rows = pl.ds(pl.multiple_of(c * OUT_STEP, OUT_STEP), OUT_STEP)
        z = []
        for parity in range(2):
            pieces = []
            for half in range(2):
                at = pl.ds((2 * parity + half) * LANES, LANES)
                x = coef[rows, at][:, None, :] * spread[own, at][None]
                x = x.reshape(OUT_STEP * ROWS, LANES)
                hi = x.astype(BF16)
                if half == 1:
                    hi = hi.astype(F32)
                    hi = jnp.where(lane < SPLIT, x - hi, hi).astype(BF16)
                pieces.append(hi)
            z.append(
                jnp.dot(
                    jnp.concatenate(pieces, -1), bwd[parity], preferred_element_type=F32
                )
            )
        both = jnp.concatenate([z[0] + z[1], z[0] - z[1]], -1)
        held[rows] = both.reshape(OUT_STEP, ROWS, NPHI)
        pltpu.make_async_copy(held.at[rows], out.at[rows], out_sem.at[0]).start()
        return 0

    lax.fori_loop(0, steps, chunk, 0)
    pltpu.make_async_copy(held, out, out_sem.at[0]).wait()


def body(density):
    forward, backward, local, spread = (jnp.asarray(t) for t in tables())
    hbm = pl.BlockSpec(memory_space=pltpu.HBM)
    vmem = pl.BlockSpec(memory_space=pltpu.VMEM)
    dma = pltpu.SemaphoreType.DMA
    wide = 2 * LANES
    coef = pl.pallas_call(
        analyse,
        out_shape=jax.ShapeDtypeStruct((FIELDS * SHELLS, 2 * wide), F32),
        in_specs=[hbm] * 3,
        out_specs=vmem,
        scratch_shapes=[
            pltpu.VMEM((FIELDS, SHELLS, ROWS, NPHI), F32),
            pltpu.VMEM((2, HALF, wide), BF16),
            pltpu.VMEM((ROWS + 8, wide), F32),
            pltpu.VMEM((4, SHELLS, wide), F32),
            pltpu.VMEM((2, SHELLS, 2 * wide), F32),
            pltpu.VMEM((FIELDS, NANG, GROUP, wide), F32),
            pltpu.VMEM((FIELDS, NANG, GROUP, wide), F32),
            pltpu.VMEM((FIELDS, GROUP, wide), F32),
            pltpu.VMEM((FIELDS, NANG, GROUP, wide), F32),
            pltpu.VMEM((FIELDS, SHELLS, 2 * wide), F32),
            pltpu.VMEM((2, 4, wide), F32),
            pltpu.VMEM((NRAD, 4, wide), F32),
            pltpu.VMEM((2, 4, wide), F32),
            pltpu.VMEM((NANG, 2, 4, wide), F32),
            dma((AHEAD + 1,)),
            dma((2,)),
            dma((FIELDS,)),
            dma((FIELDS,)),
            dma((1,)),
            dma((1,)),
            dma((4,)),
        ],
        compiler_params=pltpu.CompilerParams(
            collective_id=0, has_side_effects=True, vmem_limit_bytes=40 << 20
        ),
        name="analyse",
    )(*[pltpu.with_memory_space_constraint(x, pltpu.HBM) for x in (density, forward, local)])
    potential = pl.pallas_call(
        synthesise,
        out_shape=jax.ShapeDtypeStruct((FIELDS * SHELLS, ROWS, NPHI), F32),
        in_specs=[vmem, vmem, vmem],
        out_specs=hbm,
        scratch_shapes=[
            pltpu.VMEM((FIELDS * SHELLS, ROWS, NPHI), F32),
            dma((1,)),
        ],
        compiler_params=pltpu.CompilerParams(vmem_limit_bytes=40 << 20),
        name="synthesise",
    )(coef, backward, spread)
    return potential.reshape(FIELDS, SHELLS, ROWS, NPHI)


def solution(mesh):
    return jax.shard_map(
        body,
        mesh=mesh,
        in_specs=(P(None, "rad", "ang", None),),
        out_specs=P(None, "rad", "ang", None),
        check_vma=False,
    )
```

time: 31.9 us -> 26.4 us (0.83)
  Pallas kernels: 31.8 us -> 26.2 us
    pallas_call x1, Pallas kernels: 26.4 us -> 21.3 us  [body(): pl.pallas_call(analyse, out_shape=jax.ShapeDtypeStruct((FIELDS * SHELLS,...]
    pallas_call x1, Pallas kernels: 5.37 us -> 4.88 us  [body(): pl.pallas_call(synthesise, out_shape=jax.ShapeDtypeStruct((FIELDS * SHELL...]
where the time goes in v2:
time: 26.4 us; the launch traced here: 26.3 us
  Pallas kernels  26.2 us (99%)
    pallas_call x1, Pallas kernels, body(): pl.pallas_call(analyse, out_shape=jax.ShapeDtypeStruct((FIELDS * SHELLS,...  21.3 us
    pallas_call x1, Pallas kernels, body(): pl.pallas_call(synthesise, out_shape=jax.ShapeDtypeStruct((FIELDS * SHELL...  4.88 us

profile of v2, /device:TPU:1, one launch (start us, length us, event | category | flops | bytes accessed | tf_op | source)
XLA Modules:
  0.0 26.3 jit_solution(9316751827529019199)
XLA Ops:
  0.0 0.0 copy-start
  0.0 0.0 copy-start.1
  0.0 21.3 %analyse.1.coef = f32[192,512]{1,0:T(8,128)S(1)} custom-call(f32[3,64,32,512]{3,2,1,0:T(8,128)} %dens.1, bf16[2,256,256]{2,1,0:T(8,128)(2,1)} %constant.8.clone.forward, f32[8,40,256]{2,1,0:T(8,128)} %constant.10.clone.local), custom_call_target="tpu_custom_call" | custom-call | tf_op jit(solution)/shard_map/analyse/pallas_call | solution.py:407
  21.4 0.0 copy-done
  21.4 0.0 copy-done.1
  21.4 4.9 %synthesise.1 = f32[192,32,512]{2,1,0:T(8,128)} custom-call(f32[192,512]{1,0:T(8,128)S(1)} %analyse.1.coef, bf16[2,256,256]{2,1,0:T(8,128)(2,1)S(1)} %copy-done.1, f32[256,512]{1,0:T(8,128)S(1)} %copy-done), custom_call_target="tpu_custom_call" | custom-call | tf_op jit(solution)/shard_map/synthesise/pallas_call | solution.py:440
Async XLA Ops:
  0.0 21.4 %copy-start = (f32[256,512]{1,0:T(8,128)S(1)}, f32[256,512]{1,0:T(8,128)}, u32[]{:S(2)}) copy-start(f32[256,512]{1,0:T(8,128)} %constant.11.clone.spread) | copy-start | bytes 1572868
  0.0 21.4 %copy-start.1 = (bf16[2,256,256]{2,1,0:T(8,128)(2,1)S(1)}, bf16[2,256,256]{2,1,0:T(8,128)(2,1)}, u32[]{:S(2)}) copy-start(bf16[2,256,256]{2,1,0:T(8,128)(2,1)} %constant.9.clone.bwd) | copy-start | bytes 786436
